TPU v7x, 32 devices: a whole 2x2x4 slice. The times are simulated.
32 devices in a mesh: seq: 4 (over y, x), wshard: 8 (over z, core).
Axes of the slice: x: 2, y: 2, z: 4, core: 2. Of those that a mesh axis runs over, the one named last changes fastest.
Arguments:
- layer_input: bfloat16 [8, 1024, 1536], P('wshard', 'seq'), may hold values from -6 to 6
- lengths: int32 [8], P('wshard'), may hold values from 256 to 1024, as said below
- norm_attn: float32 [1536], replicated, may hold values from 0.1 to 1.9
- w_query: bfloat16 [1536, 1536], P('wshard'), may hold values from -0.15625 to 0.15625
- w_key: bfloat16 [1536, 1536], P('wshard'), may hold values from -0.15625 to 0.15625
- w_value: bfloat16 [1536, 1536], P('wshard'), may hold values from -0.15625 to 0.15625
- w_ogate: bfloat16 [1536, 1536], P('wshard'), may hold values from -0.15625 to 0.15625
- w_forget: bfloat16 [1536, 24], P('wshard'), may hold values from -0.15625 to 0.15625
- forget_bias: float32 [24], replicated, may hold values from 3.5 to 8
- w_out: bfloat16 [1536, 1536], P('wshard'), may hold values from -1 to 1
- norm_ffn: float32 [1536], replicated, may hold values from 0.1 to 1.9
- w_gate: bfloat16 [1536, 4096], P('wshard'), may hold values from -0.15625 to 0.15625
- w_up: bfloat16 [1536, 4096], P('wshard'), may hold values from -0.15625 to 0.15625
- w_down: bfloat16 [4096, 1536], P('wshard'), may hold values from -0.09375 to 0.09375
- output_grad: bfloat16 [8, 1024, 1536], P('wshard', 'seq'), may hold values from -6 to 6
Outputs:
- layer_output: bfloat16 [8, 1024, 1536], P('wshard', 'seq')
- grad_input: float32 [8, 1024, 1536], P('wshard', 'seq')
- grad_norm_attn: float32 [1536], replicated
- grad_w_query: float32 [1536, 1536], P('wshard')
- grad_w_key: float32 [1536, 1536], P('wshard')
- grad_w_value: float32 [1536, 1536], P('wshard')
- grad_w_ogate: float32 [1536, 1536], P('wshard')
- grad_w_forget: float32 [1536, 24], P('wshard')
- grad_forget_bias: float32 [24], replicated
- grad_w_out: float32 [1536, 1536], P('wshard')
- grad_norm_ffn: float32 [1536], replicated
- grad_w_gate: float32 [1536, 4096], P('wshard')
- grad_w_up: float32 [1536, 4096], P('wshard')
- grad_w_down: float32 [4096, 1536], P('wshard')
Inputs may be any that keep to these rules, and one draw needn't show every extreme that they name: Each sequence has 1024 slots of which the first lengths[s] are valid; in every draw one sequence is full and one has exactly 256 valid slots.
All inputs are finite; a program needn't handle non-finite values.
Results may differ from a plain program's by a relative error of at most 0.014.
Values may be sent and summed in bfloat16 or wider, within the bound.
A program may use at most 320 MiB of HBM per device.

v0:
```python
import jax
import jax.numpy as jnp
from jax import lax
from jax.sharding import PartitionSpec as P

EPS = 1e-06
NEG_FILL = -1e30
BF16 = jnp.bfloat16
F32 = jnp.float32


def product(left, right):
    return jnp.dot(left, right, preferred_element_type=F32)


def product_tn(left, right):
    return lax.dot_general(left, right, (((0,), (0,)), ((), ())), preferred_element_type=F32)


def product_nt(left, right):
    return lax.dot_general(left, right, (((1,), (1,)), ((), ())), preferred_element_type=F32)


def rms_norm(values, gain):
    return values * lax.rsqrt(jnp.mean(values * values, axis=-1, keepdims=True) + EPS) * gain


def gate_product(attended, gate_pre):
    return attended * jax.nn.sigmoid(gate_pre)


def swiglu(gate, upward):
    return jax.nn.silu(gate) * upward


def gather_rows(shard):
    return lax.all_gather(shard, "wshard", axis=0, tiled=True)


def scatter_rows(partial):
    return lax.psum_scatter(partial.astype(BF16), "wshard", scatter_dimension=0, tiled=True)


def gather_slots(shard):
    return lax.all_gather(shard, "seq", axis=0, tiled=True)


def scatter_slots(partial):
    return lax.psum_scatter(partial.astype(BF16), "seq", scatter_dimension=0, tiled=True).astype(
        F32
    )


def share_columns(share):
    return lax.all_gather(share, "seq", axis=1, tiled=True).astype(F32)


def block_scores(query_block, key_block, cum_rows, cum_keys, first_row, length, scale):
    plain = jnp.einsum("qhd,khd->hqk", query_block, key_block, preferred_element_type=F32) * scale
    plain = plain + cum_rows.T[:, :, None] - cum_keys.T[:, None, :]
    rows = first_row + jnp.arange(query_block.shape[0], dtype=jnp.int32)
    columns = jnp.arange(key_block.shape[0], dtype=jnp.int32)
    allowed = (columns[None, :] <= rows[:, None]) & (columns[None, :] < length)
    return jnp.where(allowed[None], plain, NEG_FILL)


def attention_forward(query, key, value, cumulative, length, scale, block):
    slots = query.shape[0]
    blocks = []
    log_totals = []
    for first in range(0, slots, block):
        last = first + block
        masked = block_scores(
            query[first:last],
            key[:last],
            cumulative[first:last],
            cumulative[:last],
            first,
            length,
            scale,
        )
        log_total = jax.nn.logsumexp(masked, axis=-1, keepdims=True)
        probability = jnp.exp(masked - log_total).astype(BF16)
        blocks.append(
            jnp.einsum("hqk,khd->qhd", probability, value[:last], preferred_element_type=F32)
        )
        log_totals.append(log_total)
    return (jnp.concatenate(blocks, axis=0).astype(BF16), log_totals)


def attention_backward(query, key, value, grad, cumulative, log_totals, length, scale, block):
    slots, heads, size = query.shape
    grad_query = []
    grad_key = jnp.zeros((slots, heads, size), F32)
    grad_value = jnp.zeros((slots, heads, size), F32)
    grad_cum = jnp.zeros((slots, heads), F32)
    for number, first in enumerate(range(0, slots, block)):
        last = first + block
        masked = block_scores(
            query[first:last],
            key[:last],
            cumulative[first:last],
            cumulative[:last],
            first,
            length,
            scale,
        )
        probability = jnp.exp(masked - log_totals[number])
        probability_low = probability.astype(BF16)
        grad_block = grad[first:last]
        grad_probability = jnp.einsum(
            "qhd,khd->hqk", grad_block, value[:last], preferred_element_type=F32
        )
        row_dot = jnp.sum(grad_probability * probability, axis=-1, keepdims=True)
        score_terms = probability * (grad_probability - row_dot)
        grad_scores = score_terms.astype(BF16)
        grad_cum = grad_cum.at[first:last].add(jnp.sum(score_terms, axis=2).T)
        grad_cum = grad_cum.at[:last].add(-jnp.sum(score_terms, axis=1).T)
        grad_query.append(
            jnp.einsum("hqk,khd->qhd", grad_scores, key[:last], preferred_element_type=F32)
        )
        grad_key = grad_key.at[:last].add(
            jnp.einsum("hqk,qhd->khd", grad_scores, query[first:last], preferred_element_type=F32)
        )
        grad_value = grad_value.at[:last].add(
            jnp.einsum("hqk,qhd->khd", probability_low, grad_block, preferred_element_type=F32)
        )
    grad_query = (jnp.concatenate(grad_query, axis=0) * scale).astype(BF16)
    return (grad_query, (grad_key * scale).astype(BF16), grad_value.astype(BF16), grad_cum)


def on_device(
    layer_input,
    lengths,
    norm_attn,
    w_query,
    w_key,
    w_value,
    w_ogate,
    w_forget,
    forget_bias,
    w_out,
    norm_ffn,
    w_gate,
    w_up,
    w_down,
    output_grad,
):
    tokens, width = layer_input.shape[1:]
    heads = forget_bias.shape[0]
    groups = lax.axis_size("seq")
    owners = lax.axis_size("wshard")
    local_heads = heads // groups
    head_size = width // heads
    slots = tokens * groups
    part = width // groups
    units = w_gate.shape[1]
    own_units = units // owners
    piece = own_units // groups
    local_units = units // groups
    block = min(512, slots)
    scale = head_size ** (-0.5)
    length = lengths[0]
    rank = lax.axis_index("seq")
    positions = rank * tokens + jnp.arange(tokens, dtype=jnp.int32)
    valid_slots = (positions < length).astype(F32)[:, None]
    inputs = layer_input[0].astype(F32)
    cotangent = output_grad[0].astype(F32) * valid_slots

    def columns(weight):
        return lax.dynamic_slice_in_dim(weight, rank * part, part, 1)

    def unit_columns(weight):
        cut = lax.dynamic_index_in_dim(
            weight.reshape(-1, owners, groups, piece), rank, 2, keepdims=False
        )
        return cut.reshape(-1, local_units)

    pad = -local_heads % 128
    forget_columns = jnp.pad(
        lax.dynamic_slice_in_dim(w_forget, rank * local_heads, local_heads, 1), ((0, 0), (0, pad))
    )
    normed_attn = gather_slots(rms_norm(inputs, norm_attn).astype(BF16))
    full_attn = gather_rows(
        jnp.concatenate(
            [columns(w_query), columns(w_key), columns(w_value), columns(w_ogate), forget_columns],
            axis=1,
        )
    )
    cut_out = gather_rows(columns(w_out))
    full_out = lax.all_to_all(cut_out, "seq", split_axis=0, concat_axis=1, tiled=True)
    full_gate_up = gather_rows(jnp.concatenate([unit_columns(w_gate), unit_columns(w_up)], axis=1))
    full_down = gather_rows(lax.dynamic_slice_in_dim(w_down, rank * piece, piece, 0))
    cotangent_low = gather_slots(cotangent.astype(BF16))
    query = product(normed_attn, full_attn[:, :part]).astype(BF16)
    key = product(normed_attn, full_attn[:, part : 2 * part]).astype(BF16)
    value = product(normed_attn, full_attn[:, 2 * part : 3 * part]).astype(BF16)
    gate_pre = product(normed_attn, full_attn[:, 3 * part : 4 * part])
    forget_pre = product(normed_attn, full_attn[:, 4 * part :])[:, :local_heads].astype(BF16)
    query = query.reshape(slots, local_heads, head_size)
    key = key.reshape(slots, local_heads, head_size)
    value = value.reshape(slots, local_heads, head_size)
    bias_local = lax.dynamic_slice_in_dim(forget_bias, rank * local_heads, local_heads)
    forget_total = forget_pre.astype(F32) + bias_local
    log_forget, pull_forget = jax.vjp(jax.nn.log_sigmoid, forget_total)
    cumulative = jnp.cumsum(log_forget, axis=0)
    head_output, log_totals = attention_forward(query, key, value, cumulative, length, scale, block)
    attended = head_output.reshape(slots, part).astype(F32)
    gated_full, pull_gate = jax.vjp(gate_product, attended, gate_pre)
    gated = gated_full.astype(BF16)
    middle = inputs + scatter_slots(product(gated, full_out))
    normed_ffn_full, pull_ffn_norm = jax.vjp(rms_norm, middle, norm_ffn)
    normed_ffn = gather_slots(normed_ffn_full.astype(BF16))
    gate_value = product(normed_ffn, full_gate_up[:, :local_units])
    up_value = product(normed_ffn, full_gate_up[:, local_units:])
    hidden_full, pull_swiglu = jax.vjp(swiglu, gate_value, up_value)
    hidden = hidden_full.astype(BF16)
    result = middle + scatter_slots(product(hidden, full_down))
    layer_output = result.astype(BF16)[None]
    grad_hidden = product_nt(cotangent_low, full_down)
    grad_gate_full, grad_up_full = pull_swiglu(grad_hidden)
    grad_gate_up = jnp.concatenate([grad_gate_full.astype(BF16), grad_up_full.astype(BF16)], axis=1)
    grad_normed_ffn = scatter_slots(product_nt(grad_gate_up, full_gate_up))
    share_down = scatter_rows(product_tn(hidden, cotangent_low))
    share_gate_up = scatter_rows(product_tn(normed_ffn, grad_gate_up))
    grad_middle_part, grad_norm_ffn = pull_ffn_norm(grad_normed_ffn)
    grad_middle = cotangent + grad_middle_part
    grad_branch = gather_slots(grad_middle.astype(BF16))
    grad_gated = product_nt(grad_branch, full_out)
    grad_w_out = product_tn(gated, grad_branch).astype(BF16)
    share_out = scatter_rows(
        lax.all_to_all(grad_w_out, "seq", split_axis=1, concat_axis=0, tiled=True)
    )
    grad_attended_full, grad_gate_pre_full = pull_gate(grad_gated)
    grad_attended = grad_attended_full.astype(BF16).reshape(slots, local_heads, head_size)
    grad_gate_pre = grad_gate_pre_full.astype(BF16)
    grad_query, grad_key, grad_value, grad_cum = attention_backward(
        query, key, value, grad_attended, cumulative, log_totals, length, scale, block
    )
    grad_log_forget = jnp.flip(jnp.cumsum(jnp.flip(grad_cum, 0), axis=0), 0)
    grad_forget_total = pull_forget(grad_log_forget)[0]
    grad_bias_local = jnp.sum(grad_forget_total, axis=0)
    grad_bias = lax.dynamic_update_slice_in_dim(
        jnp.zeros((heads,), F32), grad_bias_local, rank * local_heads, 0
    )
    grad_attn = jnp.concatenate(
        [
            grad_query.reshape(slots, part),
            grad_key.reshape(slots, part),
            grad_value.reshape(slots, part),
            grad_gate_pre,
            jnp.pad(grad_forget_total.astype(BF16), ((0, 0), (0, pad))),
        ],
        axis=1,
    )
    grad_normed_attn = scatter_slots(product_nt(grad_attn, full_attn))
    share_attn = scatter_rows(product_tn(normed_attn, grad_attn))
    unused_normed, pull_attn_norm = jax.vjp(rms_norm, inputs, norm_attn)
    grad_input_part, grad_norm_attn = pull_attn_norm(grad_normed_attn)
    grad_input = (grad_middle + grad_input_part)[None]
    rows = w_query.shape[0]
    all_down = lax.all_gather(share_down, "seq", axis=0, tiled=True).astype(F32)
    all_gate_up = lax.all_gather(share_gate_up, "seq", axis=0, tiled=False)
    all_gate_up = all_gate_up.reshape(groups, rows, 2, owners, piece).transpose(2, 1, 3, 0, 4)
    all_gate_up = all_gate_up.reshape(2, rows, units).astype(F32)
    all_out = share_columns(share_out)
    all_attn = lax.all_gather(share_attn, "seq", axis=0, tiled=False)

    def whole(first, size):
        cut = all_attn[:, :, first : first + size].transpose(1, 0, 2)
        return cut.reshape(rows, groups * size).astype(F32)

    small = lax.psum((grad_norm_attn, grad_norm_ffn, grad_bias), ("seq", "wshard"))
    return (
        layer_output,
        grad_input,
        small[0],
        whole(0, part),
        whole(part, part),
        whole(2 * part, part),
        whole(3 * part, part),
        whole(4 * part, local_heads),
        small[2],
        all_out,
        small[1],
        all_gate_up[0],
        all_gate_up[1],
        all_down,
    )


def solution(mesh):
    rows = P("wshard", None)
    slots = P("wshard", "seq", None)
    return jax.shard_map(
        on_device,
        mesh=mesh,
        in_specs=(
            slots,
            P("wshard"),
            P(),
            rows,
            rows,
            rows,
            rows,
            rows,
            P(),
            rows,
            P(),
            rows,
            rows,
            rows,
            slots,
        ),
        out_specs=(
            slots,
            slots,
            P(),
            rows,
            rows,
            rows,
            rows,
            rows,
            P(),
            rows,
            P(),
            rows,
            rows,
            rows,
        ),
        check_vma=False,
    )
```

profile of v0, /device:TPU:0, one launch (start us, length us, event | category | flops | bytes accessed | tf_op | source)
XLA Modules:
  0.0 979.0 jit_solution(494081339802589565)
XLA Ops:
  19.4 16.4 %all-gather.18.cloned.1.call-done = bf16[1536,384]{1,0:T(8,128)(2,1)} async-done(((bf16[192,384]{1,0:T(8,128)(2,1)}), bf16[1536,384]{1,0:T(8,128)(2,1)}) %all-gather.18.cloned.1.call-update) | async-done | bytes 1179664 | tf_op jit(solution)/shard_map/all_gather | solution.py:37
  35.8 3.5 all-to-all-start
  41.4 21.1 %all-to-all-done = bf16[4,384,384]{2,1,0:T(8,128)(2,1)S(1)} async-done(((bf16[4,384,384]{2,1,0:T(8,128)(2,1)}), bf16[4,384,384]{2,1,0:T(8,128)(2,1)S(1)}, u32[]{:S(2)}, u32[]{:S(2)}) %all-to-all-start) | async-done | bytes 1179680 | tf_op jit(solution)/shard_map/all_to_all | solution.py:191
  64.0 23.1 %all-gather.14.cloned.1.call-done = bf16[1024,1536]{1,0:T(8,128)(2,1)} async-done(((bf16[256,1536]{1,0:T(8,128)(2,1)}), bf16[1024,1536]{1,0:T(8,128)(2,1)}) %all-gather.14.cloned.1.call-update) | async-done | bytes 3145744 | tf_op jit(solution)/shard_map/all_gather | solution.py:45
  87.0 57.1 %all-gather.16.cloned.1.call-done = bf16[1536,1664]{1,0:T(8,128)(2,1)} async-done(((bf16[192,1664]{1,0:T(8,128)(2,1)}), bf16[1536,1664]{1,0:T(8,128)(2,1)}) %all-gather.16.cloned.1.call-update) | async-done | bytes 5111824 | tf_op jit(solution)/shard_map/all_gather | solution.py:37
  150.3 3.8 convolution_convert_fusion.8
  163.4 3.6 fusion.86
  184.8 4.1 reshape.507
  191.2 6.7 dynamic-slice_reduce_fusion
  199.1 25.4 %reduce-scatter.9.cloned.1.call-done = bf16[256,1536]{1,0:T(8,128)(2,1)} async-done(((bf16[1024,1536]{1,0:T(8,128)(2,1)}), bf16[256,1536]{1,0:T(8,128)(2,1)}) %reduce-scatter.9.cloned.1.call-update) | async-done | bytes 786448 | tf_op jit(solution)/shard_map/reduce_scatter | solution.py:49
  228.6 42.0 %all-gather.26.cloned.1.call-done = bf16[1024,1536]{1,0:T(8,128)(2,1)} async-done(((bf16[256,1536]{1,0:T(8,128)(2,1)}), bf16[1024,1536]{1,0:T(8,128)(2,1)}) %all-gather.26.cloned.1.call-update) | async-done | bytes 3145744 | tf_op jit(solution)/shard_map/all_gather | solution.py:45
  270.7 40.3 %all-gather.24.cloned.1.call-done = bf16[1024,1536]{1,0:T(8,128)(2,1)} async-done(((bf16[128,1536]{1,0:T(8,128)(2,1)}), bf16[1024,1536]{1,0:T(8,128)(2,1)}) %all-gather.24.cloned.1.call-update) | async-done | bytes 3145744 | tf_op jit(solution)/shard_map/all_gather | solution.py:37
  311.0 8.2 fusion.88
  319.2 57.6 %all-gather.22.cloned.1.call-done = bf16[1536,2048]{1,0:T(8,128)(2,1)} async-done(((bf16[192,2048]{1,0:T(8,128)(2,1)}), bf16[1536,2048]{1,0:T(8,128)(2,1)}) %all-gather.22.cloned.1.call-update) | async-done | bytes 6291472 | tf_op jit(solution)/shard_map/all_gather | solution.py:37
  376.8 44.9 %all-gather.20.cloned.1.call-done = bf16[1024,1536]{1,0:T(8,128)(2,1)} async-done(((bf16[256,1536]{1,0:T(8,128)(2,1)}), bf16[1024,1536]{1,0:T(8,128)(2,1)}) %all-gather.20.cloned.1.call-update) | async-done | bytes 3145744 | tf_op jit(solution)/shard_map/all_gather | solution.py:45
  421.8 8.5 fusion.6
  430.3 8.5 fusion.4
  440.1 9.4 convolution_convert_fusion.2
  450.0 43.6 %reduce-scatter.13.cloned.1.call-done = bf16[256,1536]{1,0:T(8,128)(2,1)} async-done(((bf16[1024,1536]{1,0:T(8,128)(2,1)}), bf16[256,1536]{1,0:T(8,128)(2,1)}) %reduce-scatter.13.cloned.1.call-update) | async-done | bytes 786448 | tf_op jit(solution)/shard_map/reduce_scatter | solution.py:49
  498.8 7.6 convolution_convert_fusion.5
  506.5 11.6 %convolution_convert_fusion.1 = bf16[1536,2048]{1,0:T(8,128)(2,1)} fusion(bf16[1024,1536]{1,0:T(8,128)(2,1)} %all-gather.20.cloned.1.call-done, bf16[1024,1024]{0,1:T(8,128)(2,1)} %get-tuple-element.150, bf16[1024,1024]{0,1:T(8,128)(2,1)} %copy-done.58), kind=kOutput, calls=%fused_computation.7 | convolution fusion | flops 6453985280 | bytes 13631488 | tf_op jit(solution)/shard_map/dot_general | solution.py:17
  518.2 24.6 %all-gather.28.cloned.1.call-done = bf16[1024,1536]{1,0:T(8,128)(2,1)} async-done(((bf16[256,1536]{1,0:T(8,128)(2,1)}), bf16[1024,1536]{1,0:T(8,128)(2,1)}) %all-gather.28.cloned.1.call-update) | async-done | bytes 3145744 | tf_op jit(solution)/shard_map/all_gather | solution.py:45
  542.7 5.3 multiply_convert_fusion.2
  548.8 4.6 multiply_reduce_fusion.1
  553.4 5.2 fusion.80
  558.7 4.4 multiply_reduce_fusion
  563.1 5.7 fusion.79
  577.2 5.3 fusion.12
  594.7 7.9 convolution_convert_fusion
  603.3 3.8 convolution_convert_fusion.7
  607.3 18.7 %all_to_all.38 = bf16[384,4,384]{2,0,1:T(8,128)(2,1)} all-to-all(bf16[384,4,384]{2,0,1:T(8,128)(2,1)S(1)} %bitcast.215), channel_id=1, replica_groups=mesh['seq'=4,'wshard'=8] {'seq'}, dimensions={1} | all-to-all | bytes 2359296 | tf_op jit(solution)/shard_map/all_to_all | solution.py:232
  626.0 31.2 %reduce-scatter.21.cloned.1.call-done = bf16[192,2048]{1,0:T(8,128)(2,1)} async-done(((bf16[1536,2048]{1,0:T(8,128)(2,1)}), bf16[192,2048]{1,0:T(8,128)(2,1)}) %reduce-scatter.21.cloned.1.call-update) | async-done | bytes 786448 | tf_op jit(solution)/shard_map/reduce_scatter | solution.py:41
  657.3 10.2 %convolution_convert_fusion.3 = bf16[1024,1536]{1,0:T(8,128)(2,1)} fusion(bf16[1024,1664]{0,1:T(8,128)(2,1)} %copy-done.36, bf16[1536,1664]{1,0:T(8,128)(2,1)} %all-gather.16.cloned.1.call-done), kind=kOutput, calls=%fused_computation.25 | convolution fusion | flops 5236064256 | bytes 11665408 | tf_op jit(solution)/shard_map/dot_general | solution.py:21
  667.5 7.7 convolution_convert_fusion.6
  675.3 41.0 %reduce-scatter.17.cloned.1.call-done = bf16[192,1664]{1,0:T(8,128)(2,1)} async-done(((bf16[1536,1664]{1,0:T(8,128)(2,1)}), bf16[192,1664]{1,0:T(8,128)(2,1)}) %reduce-scatter.17.cloned.1.call-update) | async-done | bytes 638992 | tf_op jit(solution)/shard_map/reduce_scatter | solution.py:41
  716.3 31.0 %all-gather.30.cloned.1.call-done = bf16[512,1536]{1,0:T(8,128)(2,1)} async-done(((bf16[128,1536]{1,0:T(8,128)(2,1)}), bf16[512,1536]{1,0:T(8,128)(2,1)}) %all-gather.30.cloned.1.call-update) | async-done | bytes 1572880 | tf_op jit(solution)/shard_map/all_gather | solution.py:262
  750.9 31.5 %reduce-scatter.19.cloned.1.call-done = bf16[192,384]{1,0:T(8,128)(2,1)} async-done(((bf16[1536,384]{1,0:T(8,128)(2,1)}), bf16[192,384]{1,0:T(8,128)(2,1)}) %reduce-scatter.19.cloned.1.call-update) | async-done | bytes 147472 | tf_op jit(solution)/shard_map/reduce_scatter | solution.py:41
  782.5 14.6 %all_gather.52 = bf16[192,1536]{1,0:T(8,128)(2,1)S(1)} all-gather(bf16[192,384]{1,0:T(8,128)(2,1)} %reduce-scatter.19.cloned.1.call-done), channel_id=1, replica_groups=mesh['seq'=4,'wshard'=8] {'seq'}, dimensions={1}, use_global_device_ids=true | all-gather | bytes 737280 | tf_op jit(solution)/shard_map/all_gather | solution.py:55
  798.3 28.1 %all-gather.34.cloned.1.call-done = bf16[768,2048]{1,0:T(8,128)(2,1)} async-done(((bf16[192,2048]{1,0:T(8,128)(2,1)}), bf16[768,2048]{1,0:T(8,128)(2,1)}) %all-gather.34.cloned.1.call-update) | async-done | bytes 3145744 | tf_op jit(solution)/shard_map/all_gather | solution.py:263
  832.7 3.8 copy.88
  836.4 5.0 squeeze.16
  841.5 5.7 copy.87
  847.2 5.3 squeeze.15
  852.5 20.6 %reduce-scatter.15.cloned.1.call-done = bf16[256,1536]{1,0:T(8,128)(2,1)} async-done(((bf16[1024,1536]{1,0:T(8,128)(2,1)}), bf16[256,1536]{1,0:T(8,128)(2,1)}) %reduce-scatter.15.cloned.1.call-update) | async-done | bytes 786448 | tf_op jit(solution)/shard_map/reduce_scatter | solution.py:49
  875.0 40.3 %all-reduce.5 = (f32[1536]{0:T(1024)}, f32[24]{0:T(128)}, f32[1536]{0:T(1024)}) all-reduce(f32[1536]{0:T(1024)S(1)} %get-tuple-element.140, f32[24]{0:T(128)S(1)} %negate_dynamic-update-slice_fusion, f32[1536]{0:T(1024)S(1)} %copy-done.41), channel_id=1, replica_groups=mesh['seq'=4,'wshard'=8] {'seq','wshard'}, use_global_device_ids=true, to_apply=%region_23.24 | all-reduce | flops 3096 | bytes 24768 | tf_op jit(solution)/shard_map/psum | solution.py:273
  915.4 5.4 reduce-scatter.11.cloned.1.call-done
  920.7 4.0 fusion.32
  924.7 36.9 %all-gather.32.cloned.1.call-done = bf16[768,1664]{1,0:T(8,128)(2,1)} async-done(((bf16[192,1664]{1,0:T(8,128)(2,1)}), bf16[768,1664]{1,0:T(8,128)(2,1)}) %all-gather.32.cloned.1.call-update) | async-done | bytes 2555920 | tf_op jit(solution)/shard_map/all_gather | solution.py:267
  (281 shorter events, 107.8 us)
Async XLA Ops:
  7.2 176.7 %copy-start = (bf16[512,1536]{1,0:T(8,128)(2,1)S(1)}, bf16[512,1536]{1,0:T(8,128)(2,1)}, u32[]{:S(2)}) copy-start(bf16[512,1536]{1,0:T(8,128)(2,1)} %param.50) | copy-start | bytes 4718596
  7.2 28.6 %all-gather.18.cloned.1.call-start = ((), (), s32[]{:S(2)}) async-start(), calls=%async_computation.12 | async-start | bytes 1327104 | tf_op jit(solution)/shard_map/all_gather | solution.py:37
  9.0 78.1 %all-gather.14.cloned.1.call-start = ((), (), s32[]{:S(2)}) async-start(), calls=%async_computation.10 | async-start | bytes 3932160 | tf_op jit(solution)/shard_map/all_gather | solution.py:45
  11.5 28.5 %copy-start.56 = (f32[24]{0:T(128)S(1)}, f32[24]{0:T(128)}, u32[]{:S(2)}) copy-start(f32[24]{0:T(128)} %param.45) | copy-start | bytes 292
  13.8 130.4 %all-gather.16.cloned.1.call-start = ((), (), s32[]{:S(2)}) async-start(), calls=%async_computation.11 | async-start | bytes 5750784 | tf_op jit(solution)/shard_map/all_gather | solution.py:37
  35.8 26.8 %all-to-all-start = ((bf16[4,384,384]{2,1,0:T(8,128)(2,1)}), bf16[4,384,384]{2,1,0:T(8,128)(2,1)S(1)}, u32[]{:S(2)}, u32[]{:S(2)}) async-start(bf16[4,384,384]{2,1,0:T(8,128)(2,1)} %bitcast.248), calls=%async_computation | async-start | bytes 2359296 | tf_op jit(solution)/shard_map/all_to_all | solution.py:191
  39.3 185.2 %reduce-scatter.9.cloned.1.call-start = ((), (), s32[]{:S(2)}) async-start(), calls=%async_computation.13 | async-start | bytes 3932160 | tf_op jit(solution)/shard_map/reduce_scatter | solution.py:49
  40.1 107.2 %copy-start.52 = (f32[6]{0:T(128)}, f32[6]{0:T(128)S(1)}, u32[]{:S(2)}) copy-start(f32[6]{0:T(128)S(1)} %dynamic_slice.36) | copy-start | bytes 76
  154.1 8.9 copy-start.21
  157.3 12.6 %copy-start.15 = (bf16[512,384]{0,1:T(8,128)(2,1)}, bf16[512,384]{0,1:T(8,128)(2,1)S(1)}, u32[]{:S(2)}) copy-start(bf16[512,384]{0,1:T(8,128)(2,1)S(1)} %slice.294) | copy-start | bytes 1179652
  162.0 7.9 copy-start.3
  181.7 89.0 %all-gather.26.cloned.1.call-start = ((), (), s32[]{:S(2)}) async-start(), calls=%async_computation.18 | async-start | bytes 3932160 | tf_op jit(solution)/shard_map/all_gather | solution.py:45
  182.8 313.2 %copy-start.46 = (f32[256]{0:T(256)}, f32[256]{0:T(256)S(1)}, u32[]{:S(2)}) copy-start(f32[256]{0:T(256)S(1)} %compare_convert_fusion) | copy-start | bytes 3076
  183.9 127.1 %all-gather.24.cloned.1.call-start = ((), (), s32[]{:S(2)}) async-start(), calls=%async_computation.16 | async-start | bytes 3538944 | tf_op jit(solution)/shard_map/all_gather | solution.py:37
  184.7 192.1 %all-gather.22.cloned.1.call-start = ((), (), s32[]{:S(2)}) async-start(), calls=%async_computation.15 | async-start | bytes 7077888 | tf_op jit(solution)/shard_map/all_gather | solution.py:37
  191.2 33.3 %copy-start.4 = (bf16[1,256,1536]{2,1,0:T(8,128)(2,1)S(1)}, bf16[1,256,1536]{2,1,0:T(8,128)(2,1)}, u32[]{:S(2)}) copy-start(bf16[1,256,1536]{2,1,0:T(8,128)(2,1)} %param.37) | copy-start | bytes 2359300
  197.9 28.1 %copy-start.37 = (f32[1536]{0:T(1024)S(1)}, f32[1536]{0:T(1024)}, u32[]{:S(2)}) copy-start(f32[1536]{0:T(1024)} %param.47) | copy-start | bytes 18436
  199.0 222.7 %all-gather.20.cloned.1.call-start = ((), (), s32[]{:S(2)}) async-start(), calls=%async_computation.14 | async-start | bytes 3932160 | tf_op jit(solution)/shard_map/all_gather | solution.py:45
  226.0 270.0 %copy-start.42 = (f32[256]{0:T(256)}, f32[256]{0:T(256)S(1)}, u32[]{:S(2)}) copy-start(f32[256]{0:T(256)S(1)} %fusion.73) | copy-start | bytes 3076
  228.4 265.2 %reduce-scatter.13.cloned.1.call-start = ((), (), s32[]{:S(2)}) async-start(), calls=%async_computation.19 | async-start | bytes 3932160 | tf_op jit(solution)/shard_map/reduce_scatter | solution.py:49
  421.8 8.5 copy-start.54
  421.8 8.5 copy-start.55
  421.8 8.5 copy-start.57
  449.5 44.1 %copy-start.6 = (bf16[256,1536]{1,0:T(8,128)(2,1)S(1)}, bf16[256,1536]{1,0:T(8,128)(2,1)}, u32[]{:S(2)}) copy-start(bf16[256,1536]{1,0:T(8,128)(2,1)} %reduce-scatter.9.cloned.1.call-done) | copy-start | bytes 2359300
  449.5 93.2 %all-gather.28.cloned.1.call-start = ((), (), s32[]{:S(2)}) async-start(), calls=%async_computation.20 | async-start | bytes 3932160 | tf_op jit(solution)/shard_map/all_gather | solution.py:45
  496.0 10.4 %copy-start.50 = (f32[256]{0:T(256)}, f32[256]{0:T(256)S(1)}, u32[]{:S(2)}) copy-start(f32[256]{0:T(256)S(1)} %multiply_multiply_fusion.1) | copy-start | bytes 3076
  498.7 104.0 %reduce-scatter.23.cloned.1.call-start = ((), (), s32[]{:S(2)}) async-start(), calls=%async_computation.25 | async-start | bytes 3538944 | tf_op jit(solution)/shard_map/reduce_scatter | solution.py:41
  506.4 150.8 %reduce-scatter.21.cloned.1.call-start = ((), (), s32[]{:S(2)}) async-start(), calls=%async_computation.24 | async-start | bytes 7077888 | tf_op jit(solution)/shard_map/reduce_scatter | solution.py:41
  518.1 198.2 %reduce-scatter.17.cloned.1.call-start = ((), (), s32[]{:S(2)}) async-start(), calls=%async_computation.22 | async-start | bytes 5750784 | tf_op jit(solution)/shard_map/reduce_scatter | solution.py:41
  548.8 9.8 %slice-start = ((s8[12582912]{0:T(1024)(128)(4,1)}), s8[4194304]{0:T(1024)(128)(4,1)S(1)}, s32[]{:S(2)}) async-start(s8[12582912]{0:T(1024)(128)(4,1)} %bitcast.202), calls=%async_computation.29 | async-start | bytes 8388608
  548.8 9.8 %slice-start.1 = ((s8[12582912]{0:T(1024)(128)(4,1)}), s8[4194304]{0:T(1024)(128)(4,1)S(1)}, s32[]{:S(2)}) async-start(s8[12582912]{0:T(1024)(128)(4,1)} %bitcast.202), calls=%async_computation.30 | async-start | bytes 8388608
  574.3 9.5 slice-start.8
  577.2 8.0 slice-start.6
  602.7 144.7 %all-gather.30.cloned.1.call-start = ((), (), s32[]{:S(2)}) async-start(), calls=%async_computation.26 | async-start | bytes 1966080 | tf_op jit(solution)/shard_map/all_gather | solution.py:262
  603.3 179.2 %reduce-scatter.19.cloned.1.call-start = ((), (), s32[]{:S(2)}) async-start(), calls=%async_computation.23 | async-start | bytes 1327104 | tf_op jit(solution)/shard_map/reduce_scatter | solution.py:41
  626.0 200.4 %all-gather.34.cloned.1.call-start = ((), (), s32[]{:S(2)}) async-start(), calls=%async_computation.28 | async-start | bytes 3932160 | tf_op jit(solution)/shard_map/all_gather | solution.py:263
  657.3 215.9 %reduce-scatter.15.cloned.1.call-start = ((), (), s32[]{:S(2)}) async-start(), calls=%async_computation.21 | async-start | bytes 3932160 | tf_op jit(solution)/shard_map/reduce_scatter | solution.py:49
  667.5 253.2 %reduce-scatter.11.cloned.1.call-start = ((), (), s32[]{:S(2)}) async-start(), calls=%async_computation.17 | async-start | bytes 3932160 | tf_op jit(solution)/shard_map/reduce_scatter | solution.py:49
  675.3 286.3 %all-gather.32.cloned.1.call-start = ((), (), s32[]{:S(2)}) async-start(), calls=%async_computation.27 | async-start | bytes 3194880 | tf_op jit(solution)/shard_map/all_gather | solution.py:267
  847.2 26.0 %copy-start.40 = (f32[1536]{0:T(1024)S(1)}, f32[1536]{0:T(1024)}, u32[]{:S(2)}) copy-start(f32[1536]{0:T(1024)} %param.39) | copy-start | bytes 18436
  847.2 26.0 %copy-start.45 = (f32[256]{0:T(256)S(1)}, f32[256]{0:T(256)}, u32[]{:S(2)}) copy-start(f32[256]{0:T(256)} %copy-done.44) | copy-start | bytes 3076
  847.2 27.8 %copy-start.41 = (f32[1536]{0:T(1024)S(1)}, f32[1536]{0:T(1024)}, u32[]{:S(2)}) copy-start(f32[1536]{0:T(1024)} %get-tuple-element.138) | copy-start | bytes 18436
  847.2 68.2 %copy-start.49 = (f32[256]{0:T(256)S(1)}, f32[256]{0:T(256)}, u32[]{:S(2)}) copy-start(f32[256]{0:T(256)} %copy-done.48) | copy-start | bytes 3076
  847.2 73.5 %copy-start.8 = (bf16[256,1536]{1,0:T(8,128)(2,1)S(1)}, bf16[256,1536]{1,0:T(8,128)(2,1)}, u32[]{:S(2)}) copy-start(bf16[256,1536]{1,0:T(8,128)(2,1)} %reduce-scatter.13.cloned.1.call-done) | copy-start | bytes 2359300
  847.2 73.5 %copy-start.38 = (f32[1536]{0:T(1024)S(1)}, f32[1536]{0:T(1024)}, u32[]{:S(2)}) copy-start(f32[1536]{0:T(1024)} %param.47) | copy-start | bytes 18436
  847.2 73.5 %copy-start.43 = (f32[256]{0:T(256)S(1)}, f32[256]{0:T(256)}, u32[]{:S(2)}) copy-start(f32[256]{0:T(256)} %copy-done.42) | copy-start | bytes 3076
  847.2 73.5 %copy-start.47 = (f32[256]{0:T(256)S(1)}, f32[256]{0:T(256)}, u32[]{:S(2)}) copy-start(f32[256]{0:T(256)} %copy-done.46) | copy-start | bytes 3076
  847.2 73.5 %copy-start.51 = (f32[256]{0:T(256)S(1)}, f32[256]{0:T(256)}, u32[]{:S(2)}) copy-start(f32[256]{0:T(256)} %copy-done.50) | copy-start | bytes 3076
  (41 other events, 134.0 us)
Sparse Core Ops, SparseCore 0:
  10.2 25.4 all-gather.17
  38.2 48.8 all-gather.13
  89.3 54.8 all-gather.15
  181.8 42.6 reduce-scatter.8
  226.8 43.8 all-gather.25
  272.7 38.2 all-gather.23
  313.2 63.5 all-gather.21
  379.2 42.4 all-gather.19
  449.6 43.8 reduce-scatter.12
  498.9 43.8 all-gather.27
  545.6 40.3 reduce-scatter.22
  588.2 69.0 reduce-scatter.20
  659.6 56.7 reduce-scatter.16
  718.0 29.3 all-gather.29
  749.5 32.9 reduce-scatter.18
  784.2 42.1 all-gather.33
  829.2 43.8 reduce-scatter.14
  876.0 44.6 reduce-scatter.10
  922.6 38.9 all-gather.31
where the time goes:
time: 989 us; the launch traced here: 979 us
  waiting for transfers between devices  623 us (63%)
  matrix products  140 us (14%)
  blocking collectives  73.7 us (7%)
  local copies, waits for them, and re-layouts  68.5 us (7%)
  other arithmetic  53.1 us (5%)
  between operations  16.2 us (2%)
    all_gather x4, waiting for transfers between devices, gather_rows(): return lax.all_gather(shard, 'wshard', axis=0, tiled=True)  171 us
    all_gather x4, waiting for transfers between devices, gather_slots(): return lax.all_gather(shard, 'seq', axis=0, tiled=True)  135 us
    reduce_scatter x4, waiting for transfers between devices, scatter_rows(): lax.psum_scatter(partial.astype(BF16), 'wshard', scatter_dimension=0, til...  104 us
    reduce_scatter x4, waiting for transfers between devices, scatter_slots(): lax.psum_scatter(partial.astype(BF16), 'seq', scatter_dimension=0, tiled=...  95.1 us
    dot_general x9, matrix products, product(): return jnp.dot(left, right, preferred_element_type=F32)  44.1 us
    psum x1, blocking collectives, on_device(): lax.psum((grad_norm_attn, grad_norm_ffn, grad_bias), ('seq', 'wshard'))  40.3 us
    all_gather x1, waiting for transfers between devices, on_device(): all_attn = lax.all_gather(share_attn, 'seq', axis=0, tiled=False)  36.9 us
    dot_general x4, matrix products, product_nt(): lax.dot_general(left, right, (((1,), (1,)), ((), ())), preferred_element_...  33.1 us
  transfers between devices with their start and end apart: 20, of which 19 were waited for; matrix products, arithmetic and copies ran while one was open for 18% of the time, Pallas kernels for 0%

commit v1 on v0

--- a/solution.py
+++ b/solution.py
@@ -9,6 +9,36 @@
 F32 = jnp.float32
 
 
+def ratios_draw(xin, device_axis, pos_dim):
+    local_now = lax.axis_size(device_axis)
+    met_up, parts_out, s_next = (local_now, lax.axis_index(device_axis), xin.shape[pos_dim])
+    vals = []
+    for q in [*range(met_up)]:
+        vals.append((q, (q + 1) % met_up))
+    by_rank = []
+    for q in [*range(met_up)]:
+        by_rank.append((q, (q - 1) % met_up))
+    current_arr = jnp.zeros(
+        (*xin.shape[:pos_dim], met_up * s_next, *xin.shape[pos_dim + 1 :]), xin.dtype
+    )
+    current_arr = lax.dynamic_update_slice_in_dim(
+        current_arr, xin, parts_out * s_next, axis=pos_dim
+    )
+    upper = back = xin
+    before = met_up // 2
+    for dev_j in [*range(1, before + 1)]:
+        upper = lax.ppermute(upper, device_axis, vals)
+        current_arr = lax.dynamic_update_slice_in_dim(
+            current_arr, upper, (parts_out - dev_j) % met_up * s_next, axis=pos_dim
+        )
+        if dev_j < met_up - before:
+            back = lax.ppermute(back, device_axis, by_rank)
+            current_arr = lax.dynamic_update_slice_in_dim(
+                current_arr, back, (parts_out + dev_j) % met_up * s_next, axis=pos_dim
+            )
+    return current_arr
+
+
 def product(left, right):
     return jnp.dot(left, right, preferred_element_type=F32)
 
@@ -34,7 +64,7 @@
 
 
 def gather_rows(shard):
-    return lax.all_gather(shard, "wshard", axis=0, tiled=True)
+    return ratios_draw(shard, "wshard", pos_dim=0)
 
 
 def scatter_rows(partial):

time: 989 us -> 849 us (0.86)
  waiting for transfers between devices: 623 us -> 406 us
  local copies, waits for them, and re-layouts: 68.5 us -> 113 us
  starting transfers between devices: 4.93 us -> 46 us
    all_gather x4 -> x0, waiting for transfers between devices: 171 us -> none  [gather_rows(): return lax.all_gather(shard, 'wshard', axis=0, tiled=True)]
    all_gather x4, waiting for transfers between devices: 135 us -> 23.2 us  [gather_slots(): return lax.all_gather(shard, 'seq', axis=0, tiled=True)]
    ppermute x0 -> x28, waiting for transfers between devices: none -> 82.5 us  [the longest x16 43.9 us: ratios_draw(): upper = lax.ppermute(upper, device_axis, vals)]
    ppermute x0 -> x28, starting transfers between devices: none -> 41.7 us  [the longest x12 40.9 us: ratios_draw(): back = lax.ppermute(back, device_axis, by_rank)]
    dynamic_update_slice x0 -> x32, local copies, waits for them, and re-layouts: none -> 34.6 us  [the longest x16 16 us: ratios_draw(): lax.dynamic_update_slice_in_dim(current_arr, upper, (parts_out - dev_j) %...]
    all_to_all x1, waiting for transfers between devices: 21.1 us -> 0.01 us  [on_device(): lax.all_to_all(cut_out, 'seq', split_axis=0, concat_axis=1, tiled=True)]
    unnamed x153 -> x140, local copies, waits for them, and re-layouts: 17.9 us -> 22 us
  transfers between devices with their start and end apart: 20 -> 44, of which waited for: 19 -> 27; matrix products, arithmetic and copies ran while one was open for 18% -> 24% of each run, Pallas kernels for 0% -> 0%
where the time goes in v1:
time: 849 us; the launch traced here: 843 us
  waiting for transfers between devices  406 us (48%)
  matrix products  138 us (16%)
  local copies, waits for them, and re-layouts  113 us (13%)
  blocking collectives  73.4 us (9%)
  other arithmetic  50.8 us (6%)
  starting transfers between devices  46 us (5%)
  between operations  16 us (2%)
    reduce_scatter x4, waiting for transfers between devices, scatter_rows(): lax.psum_scatter(partial.astype(BF16), 'wshard', scatter_dimension=0, til...  108 us
    reduce_scatter x4, waiting for transfers between devices, scatter_slots(): lax.psum_scatter(partial.astype(BF16), 'seq', scatter_dimension=0, tiled=...  95.9 us
    ppermute x16, waiting for transfers between devices, ratios_draw(): upper = lax.ppermute(upper, device_axis, vals)  43.9 us
    dot_general x9, matrix products, product(): return jnp.dot(left, right, preferred_element_type=F32)  41.8 us
    ppermute x12, starting transfers between devices, ratios_draw(): back = lax.ppermute(back, device_axis, by_rank)  40.9 us
    psum x1, blocking collectives, on_device(): lax.psum((grad_norm_attn, grad_norm_ffn, grad_bias), ('seq', 'wshard'))  40.3 us
    ppermute x12, waiting for transfers between devices, ratios_draw(): back = lax.ppermute(back, device_axis, by_rank)  38.5 us
    all_gather x1, waiting for transfers between devices, on_device(): all_attn = lax.all_gather(share_attn, 'seq', axis=0, tiled=False)  36.4 us
  transfers between devices with their start and end apart: 44, of which 27 were waited for; matrix products, arithmetic and copies ran while one was open for 24% of the time, Pallas kernels for 0%

profile of v1, /device:TPU:0, one launch (start us, length us, event | category | flops | bytes accessed | tf_op | source)
XLA Modules:
  0.0 843.2 jit_solution(4040942955284742579)
XLA Ops:
  16.0 4.6 collective-permute-start.1
  32.7 6.8 collective-permute-done.7
  52.4 6.3 collective-permute-done.11
  67.3 3.7 all-to-all-start
  76.4 3.8 collective-permute-start.5
  81.1 6.9 collective-permute-done.4
  107.0 3.8 convolution_convert_fusion.8
  143.7 3.9 reshape.509
  147.6 6.6 dynamic-slice_reduce_fusion
  154.4 26.8 %reduce-scatter.9.cloned.1.call-done = bf16[256,1536]{1,0:T(8,128)(2,1)} async-done(((bf16[1024,1536]{1,0:T(8,128)(2,1)}), bf16[256,1536]{1,0:T(8,128)(2,1)}) %reduce-scatter.9.cloned.1.call-update) | async-done | bytes 786448 | tf_op jit(solution)/shard_map/reduce_scatter | solution.py:79
  205.6 10.5 %collective-permute-done.15 = bf16[192,2048]{1,0:T(8,128)(2,1)} collective-permute-done((bf16[192,2048]{1,0:T(8,128)(2,1)S(1)}, bf16[192,2048]{1,0:T(8,128)(2,1)}, u32[]{:S(2)}, u32[]{:S(2)}) %collective-permute-start.15) | collective-permute-done | bytes 786464 | tf_op jit(solution)/shard_map/ppermute | solution.py:35
  216.1 3.8 collective-permute-start.17
  219.9 4.6 collective-permute-done.24
  234.0 5.0 collective-permute-done.25
  239.8 10.0 %collective-permute-done.26 = bf16[128,1536]{1,0:T(8,128)(2,1)S(1)} collective-permute-done((bf16[128,1536]{1,0:T(8,128)(2,1)S(1)}, bf16[128,1536]{1,0:T(8,128)(2,1)S(1)}, u32[]{:S(2)}, u32[]{:S(2)}) %collective-permute-start.26) | collective-permute-done | bytes 393248 | tf_op jit(solution)/shard_map/ppermute | solution.py:35
  255.8 4.4 collective-permute-done.27
  262.8 8.4 collective-permute-done.19
  274.9 8.3 fusion.88
  283.3 6.6 fusion.6
  289.9 8.7 %fusion.4 = (bf16[1024,1024]{0,1:T(8,128)(2,1)S(1)}, bf16[1024,1024]{0,1:T(8,128)(2,1)S(1)}, bf16[1024,1024]{0,1:T(8,128)(2,1)}) fusion(f32[1024,1024]{0,1:T(8,128)S(1)} %copy-done.46, f32[1024,1024]{0,1:T(8,128)S(1)} %fusion.6, bf16[1024,1536]{1,0:T(8,128)(2,1)S(1)} %copy-done.44, bf16[1536,2048]{1,0:T(8,128)(2,1)} %constant_dynamic-update-slice_fusion.10), kind=kOutput, calls=%fused_computation.18 | convolution fusion | flops 3238002688 | bytes 20971520 | tf_op jit(solution)/shard_map/dot_general | solution.py:43
  300.6 10.1 %convolution_convert_fusion.2 = bf16[1024,1536]{1,0:T(8,128)(2,1)} fusion(bf16[1536,2048]{1,0:T(8,128)(2,1)} %constant_dynamic-update-slice_fusion.10, bf16[1024,1024]{0,1:T(8,128)(2,1)S(1)} %get-tuple-element.154, bf16[1024,1024]{0,1:T(8,128)(2,1)S(1)} %get-tuple-element.153), kind=kOutput, calls=%fused_computation.24 | convolution fusion | flops 6452412416 | bytes 13631488 | tf_op jit(solution)/shard_map/dot_general | solution.py:51
  310.7 42.7 %reduce-scatter.13.cloned.1.call-done = bf16[256,1536]{1,0:T(8,128)(2,1)} async-done(((bf16[1024,1536]{1,0:T(8,128)(2,1)}), bf16[256,1536]{1,0:T(8,128)(2,1)}) %reduce-scatter.13.cloned.1.call-update) | async-done | bytes 786448 | tf_op jit(solution)/shard_map/reduce_scatter | solution.py:79
  358.1 7.6 convolution_convert_fusion.5
  367.4 11.4 %convolution_convert_fusion.1 = bf16[1536,2048]{1,0:T(8,128)(2,1)} fusion(bf16[1024,1536]{1,0:T(8,128)(2,1)} %all-gather.12.cloned.1.call-done, bf16[1024,1024]{0,1:T(8,128)(2,1)} %copy-done.50, bf16[1024,1024]{0,1:T(8,128)(2,1)S(1)} %copy-done.49), kind=kOutput, calls=%fused_computation.7 | convolution fusion | flops 6453985280 | bytes 13631488 | tf_op jit(solution)/shard_map/dot_general | solution.py:47
  378.8 23.2 %all-gather.16.cloned.1.call-done = bf16[1024,1536]{1,0:T(8,128)(2,1)} async-done(((bf16[256,1536]{1,0:T(8,128)(2,1)}), bf16[1024,1536]{1,0:T(8,128)(2,1)}) %all-gather.16.cloned.1.call-update) | async-done | bytes 3145744 | tf_op jit(solution)/shard_map/all_gather | solution.py:75
  402.0 5.4 multiply_convert_fusion.2
  408.2 5.2 multiply_reduce_fusion.1
  416.7 4.2 multiply_reduce_fusion
  421.0 5.4 fusion.79
  432.5 5.0 fusion.12
  449.7 8.1 convolution_convert_fusion
  462.3 18.5 %all_to_all.38 = bf16[384,4,384]{2,0,1:T(8,128)(2,1)} all-to-all(bf16[384,4,384]{2,0,1:T(8,128)(2,1)S(1)} %bitcast.215), channel_id=1, replica_groups=mesh['seq'=4,'wshard'=8] {'seq'}, dimensions={1} | all-to-all | bytes 2359296 | tf_op jit(solution)/shard_map/all_to_all | solution.py:262
  480.9 35.8 %reduce-scatter.21.cloned.1.call-done = bf16[192,2048]{1,0:T(8,128)(2,1)} async-done(((bf16[1536,2048]{1,0:T(8,128)(2,1)}), bf16[192,2048]{1,0:T(8,128)(2,1)}) %reduce-scatter.21.cloned.1.call-update) | async-done | bytes 786448 | tf_op jit(solution)/shard_map/reduce_scatter | solution.py:71
  516.7 10.1 %convolution_convert_fusion.3 = bf16[1024,1536]{1,0:T(8,128)(2,1)} fusion(bf16[1024,1664]{0,1:T(8,128)(2,1)} %copy-done.35, bf16[1536,1664]{1,0:T(8,128)(2,1)} %constant_dynamic-update-slice_fusion.26), kind=kOutput, calls=%fused_computation.25 | convolution fusion | flops 5236064256 | bytes 11665408 | tf_op jit(solution)/shard_map/dot_general | solution.py:51
  528.4 6.8 convolution_convert_fusion.6
  535.3 40.8 %reduce-scatter.17.cloned.1.call-done = bf16[192,1664]{1,0:T(8,128)(2,1)} async-done(((bf16[1536,1664]{1,0:T(8,128)(2,1)}), bf16[192,1664]{1,0:T(8,128)(2,1)}) %reduce-scatter.17.cloned.1.call-update) | async-done | bytes 638992 | tf_op jit(solution)/shard_map/reduce_scatter | solution.py:71
  576.1 31.0 %all-gather.18.cloned.1.call-done = bf16[512,1536]{1,0:T(8,128)(2,1)} async-done(((bf16[128,1536]{1,0:T(8,128)(2,1)}), bf16[512,1536]{1,0:T(8,128)(2,1)}) %all-gather.18.cloned.1.call-update) | async-done | bytes 1572880 | tf_op jit(solution)/shard_map/all_gather | solution.py:292
  610.7 31.6 %reduce-scatter.19.cloned.1.call-done = bf16[192,384]{1,0:T(8,128)(2,1)} async-done(((bf16[1536,384]{1,0:T(8,128)(2,1)}), bf16[192,384]{1,0:T(8,128)(2,1)}) %reduce-scatter.19.cloned.1.call-update) | async-done | bytes 147472 | tf_op jit(solution)/shard_map/reduce_scatter | solution.py:71
  642.3 14.6 %all_gather.36 = bf16[192,1536]{1,0:T(8,128)(2,1)S(1)} all-gather(bf16[192,384]{1,0:T(8,128)(2,1)} %reduce-scatter.19.cloned.1.call-done), channel_id=1, replica_groups=mesh['seq'=4,'wshard'=8] {'seq'}, dimensions={1}, use_global_device_ids=true | all-gather | bytes 737280 | tf_op jit(solution)/shard_map/all_gather | solution.py:85
  658.0 28.3 %all-gather.22.cloned.1.call-done = bf16[768,2048]{1,0:T(8,128)(2,1)} async-done(((bf16[192,2048]{1,0:T(8,128)(2,1)}), bf16[768,2048]{1,0:T(8,128)(2,1)}) %all-gather.22.cloned.1.call-update) | async-done | bytes 3145744 | tf_op jit(solution)/shard_map/all_gather | solution.py:293
  696.2 5.0 squeeze.16
  701.2 5.6 copy.87
  706.9 5.2 squeeze.15
  712.1 21.1 %reduce-scatter.15.cloned.1.call-done = bf16[256,1536]{1,0:T(8,128)(2,1)} async-done(((bf16[1024,1536]{1,0:T(8,128)(2,1)}), bf16[256,1536]{1,0:T(8,128)(2,1)}) %reduce-scatter.15.cloned.1.call-update) | async-done | bytes 786448 | tf_op jit(solution)/shard_map/reduce_scatter | solution.py:79
  735.0 40.3 %all-reduce.5 = (f32[1536]{0:T(1024)}, f32[24]{0:T(128)}, f32[1536]{0:T(1024)}) all-reduce(f32[1536]{0:T(1024)S(1)} %get-tuple-element.140, f32[24]{0:T(128)S(1)} %negate_dynamic-update-slice_fusion, f32[1536]{0:T(1024)S(1)} %get-tuple-element.138), channel_id=1, replica_groups=mesh['seq'=4,'wshard'=8] {'seq','wshard'}, use_global_device_ids=true, to_apply=%region_23.24 | all-reduce | flops 3096 | bytes 24768 | tf_op jit(solution)/shard_map/psum | solution.py:303
  775.4 5.4 reduce-scatter.11.cloned.1.call-done
  780.8 4.3 fusion.32
  785.0 36.4 %all-gather.20.cloned.1.call-done = bf16[768,1664]{1,0:T(8,128)(2,1)} async-done(((bf16[192,1664]{1,0:T(8,128)(2,1)}), bf16[768,1664]{1,0:T(8,128)(2,1)}) %all-gather.20.cloned.1.call-update) | async-done | bytes 2555920 | tf_op jit(solution)/shard_map/all_gather | solution.py:297
  (347 shorter events, 214.7 us)
Async XLA Ops:
  7.2 93.7 %all-gather.10.cloned.1.call-start = ((), (), s32[]{:S(2)}) async-start(), calls=%async_computation.10 | async-start | bytes 3932160 | tf_op jit(solution)/shard_map/all_gather | solution.py:75
  16.0 43.4 %collective-permute-start.1 = (bf16[192,1664]{1,0:T(8,128)(2,1)S(1)}, bf16[192,1664]{1,0:T(8,128)(2,1)S(1)}, u32[]{:S(2)}, u32[]{:S(2)}) collective-permute-start(bf16[192,1664]{1,0:T(8,128)(2,1)S(1)} %pad_dynamic-update-slice_fusion.1), channel_id=1, source_target_pairs={{0,7},{1,0},{2,1},{3,2},{4,3},{5,4},{6,5},{7,6},{8,15},{9,8},{10,9... | collective-permute-start | bytes 1916936 | tf_op jit(solution)/shard_map/ppermute | solution.py:35
  20.6 23.2 %collective-permute-start = (bf16[192,1664]{1,0:T(8,128)(2,1)S(1)}, bf16[192,1664]{1,0:T(8,128)(2,1)S(1)}, u32[]{:S(2)}, u32[]{:S(2)}) collective-permute-start(bf16[192,1664]{1,0:T(8,128)(2,1)S(1)} %pad_dynamic-update-slice_fusion.1), channel_id=1, source_target_pairs={{0,1},{1,2},{2,3},{3,4},{4,5},{5,6},{6,7},{7,0},{8,9},{9,10},{10,1... | collective-permute-start | bytes 1916936 | tf_op jit(solution)/shard_map/ppermute | solution.py:30
  23.3 16.2 %collective-permute-start.7 = (bf16[192,384]{1,0:T(8,128)(2,1)S(1)}, bf16[192,384]{1,0:T(8,128)(2,1)S(1)}, u32[]{:S(2)}, u32[]{:S(2)}) collective-permute-start(bf16[192,384]{1,0:T(8,128)(2,1)S(1)} %get-tuple-element.152), channel_id=1, source_target_pairs={{0,1},{1,2},{2,3},{3,4},{4,5},{5,6},{6,7},{7,0},{8,9},{9,10},{10,1... | collective-permute-start | bytes 442376 | tf_op jit(solution)/shard_map/ppermute | solution.py:30
  23.3 16.2 %collective-permute-start.8 = (bf16[192,384]{1,0:T(8,128)(2,1)S(1)}, bf16[192,384]{1,0:T(8,128)(2,1)S(1)}, u32[]{:S(2)}, u32[]{:S(2)}) collective-permute-start(bf16[192,384]{1,0:T(8,128)(2,1)S(1)} %get-tuple-element.152), channel_id=1, source_target_pairs={{0,7},{1,0},{2,1},{3,2},{4,3},{5,4},{6,5},{7,6},{8,15},{9,8},{10,9... | collective-permute-start | bytes 442376 | tf_op jit(solution)/shard_map/ppermute | solution.py:35
  32.7 71.3 %copy-start.42 = (f32[6]{0:T(128)}, f32[6]{0:T(128)S(1)}, u32[]{:S(2)}) copy-start(f32[6]{0:T(128)S(1)} %dynamic_slice.36) | copy-start | bytes 76
  39.6 7.9 collective-permute-start.9
  39.6 7.9 collective-permute-start.10
  43.8 27.3 %collective-permute-start.2 = (bf16[192,1664]{1,0:T(8,128)(2,1)S(1)}, bf16[192,1664]{1,0:T(8,128)(2,1)S(1)}, u32[]{:S(2)}, u32[]{:S(2)}) collective-permute-start(bf16[192,1664]{1,0:T(8,128)(2,1)S(1)} %collective-permute-done), channel_id=1, source_target_pairs={{0,1},{1,2},{2,3},{3,4},{4,5},{5,6},{6,7},{7,0},{8,9},{9,10},{10,1... | collective-permute-start | bytes 1916936 | tf_op jit(solution)/shard_map/ppermute | solution.py:30
  47.5 11.2 %collective-permute-start.11 = (bf16[192,384]{1,0:T(8,128)(2,1)S(1)}, bf16[192,384]{1,0:T(8,128)(2,1)S(1)}, u32[]{:S(2)}, u32[]{:S(2)}) collective-permute-start(bf16[192,384]{1,0:T(8,128)(2,1)S(1)} %collective-permute-done.9), channel_id=1, source_target_pairs={{0,1},{1,2},{2,3},{3,4},{4,5},{5,6},{6,7},{7,0},{8,9},{9,10},{10,1... | collective-permute-start | bytes 442376 | tf_op jit(solution)/shard_map/ppermute | solution.py:30
  47.5 15.4 %collective-permute-start.12 = (bf16[192,384]{1,0:T(8,128)(2,1)S(1)}, bf16[192,384]{1,0:T(8,128)(2,1)S(1)}, u32[]{:S(2)}, u32[]{:S(2)}) collective-permute-start(bf16[192,384]{1,0:T(8,128)(2,1)S(1)} %collective-permute-done.10), channel_id=1, source_target_pairs={{0,7},{1,0},{2,1},{3,2},{4,3},{5,4},{6,5},{7,6},{8,15},{9,8},{10,9... | collective-permute-start | bytes 442376 | tf_op jit(solution)/shard_map/ppermute | solution.py:35
  58.7 7.9 collective-permute-start.13
  59.4 17.0 %collective-permute-start.3 = (bf16[192,1664]{1,0:T(8,128)(2,1)S(1)}, bf16[192,1664]{1,0:T(8,128)(2,1)}, u32[]{:S(2)}, u32[]{:S(2)}) collective-permute-start(bf16[192,1664]{1,0:T(8,128)(2,1)S(1)} %collective-permute-done.1), channel_id=1, source_target_pairs={{0,7},{1,0},{2,1},{3,2},{4,3},{5,4},{6,5},{7,6},{8,15},{9,8},{10,9... | collective-permute-start | bytes 1916936 | tf_op jit(solution)/shard_map/ppermute | solution.py:35
  67.3 22.8 %all-to-all-start = ((bf16[4,384,384]{2,1,0:T(8,128)(2,1)}), bf16[4,384,384]{2,1,0:T(8,128)(2,1)S(1)}, u32[]{:S(2)}, u32[]{:S(2)}) async-start(bf16[4,384,384]{2,1,0:T(8,128)(2,1)} %bitcast.17), calls=%async_computation | async-start | bytes 2359296 | tf_op jit(solution)/shard_map/all_to_all | solution.py:221
  71.1 110.2 %reduce-scatter.9.cloned.1.call-start = ((), (), s32[]{:S(2)}) async-start(), calls=%async_computation.11 | async-start | bytes 3932160 | tf_op jit(solution)/shard_map/reduce_scatter | solution.py:79
  71.1 16.9 %collective-permute-start.4 = (bf16[192,1664]{1,0:T(8,128)(2,1)S(1)}, bf16[192,1664]{1,0:T(8,128)(2,1)}, u32[]{:S(2)}, u32[]{:S(2)}) collective-permute-start(bf16[192,1664]{1,0:T(8,128)(2,1)S(1)} %collective-permute-done.2), channel_id=1, source_target_pairs={{0,1},{1,2},{2,3},{3,4},{4,5},{5,6},{6,7},{7,0},{8,9},{9,10},{10,1... | collective-permute-start | bytes 1916936 | tf_op jit(solution)/shard_map/ppermute | solution.py:30
  76.4 18.6 %collective-permute-start.5 = (bf16[192,1664]{1,0:T(8,128)(2,1)}, bf16[192,1664]{1,0:T(8,128)(2,1)}, u32[]{:S(2)}, u32[]{:S(2)}) collective-permute-start(bf16[192,1664]{1,0:T(8,128)(2,1)} %collective-permute-done.3), channel_id=1, source_target_pairs={{0,7},{1,0},{2,1},{3,2},{4,3},{5,4},{6,5},{7,6},{8,15},{9,8},{10,9... | collective-permute-start | bytes 1916936 | tf_op jit(solution)/shard_map/ppermute | solution.py:35
  88.0 12.0 %collective-permute-start.6 = (bf16[192,1664]{1,0:T(8,128)(2,1)}, bf16[192,1664]{1,0:T(8,128)(2,1)S(1)}, u32[]{:S(2)}, u32[]{:S(2)}) collective-permute-start(bf16[192,1664]{1,0:T(8,128)(2,1)} %collective-permute-done.4), channel_id=1, source_target_pairs={{0,1},{1,2},{2,3},{3,4},{4,5},{5,6},{6,7},{7,0},{8,9},{9,10},{10,1... | collective-permute-start | bytes 1916936 | tf_op jit(solution)/shard_map/ppermute | solution.py:30
  138.9 136.1 %all-gather.14.cloned.1.call-start = ((), (), s32[]{:S(2)}) async-start(), calls=%async_computation.14 | async-start | bytes 3932160 | tf_op jit(solution)/shard_map/all_gather | solution.py:75
  141.1 142.2 %all-gather.12.cloned.1.call-start = ((), (), s32[]{:S(2)}) async-start(), calls=%async_computation.12 | async-start | bytes 3932160 | tf_op jit(solution)/shard_map/all_gather | solution.py:75
  154.4 50.5 %collective-permute-start.14 = (bf16[192,2048]{1,0:T(8,128)(2,1)S(1)}, bf16[192,2048]{1,0:T(8,128)(2,1)}, u32[]{:S(2)}, u32[]{:S(2)}) collective-permute-start(bf16[192,2048]{1,0:T(8,128)(2,1)S(1)} %bitcast_dynamic-update-slice_fusion), channel_id=1, source_target_pairs={{0,1},{1,2},{2,3},{3,4},{4,5},{5,6},{6,7},{7,0},{8,9},{9,10},{10,1... | collective-permute-start | bytes 2359304 | tf_op jit(solution)/shard_map/ppermute | solution.py:30
  185.1 168.3 %reduce-scatter.13.cloned.1.call-start = ((), (), s32[]{:S(2)}) async-start(), calls=%async_computation.15 | async-start | bytes 3932160 | tf_op jit(solution)/shard_map/reduce_scatter | solution.py:79
  188.9 11.6 %collective-permute-start.21 = (bf16[128,1536]{1,0:T(8,128)(2,1)}, bf16[128,1536]{1,0:T(8,128)(2,1)S(1)}, u32[]{:S(2)}, u32[]{:S(2)}) collective-permute-start(bf16[128,1536]{1,0:T(8,128)(2,1)} %get-tuple-element.150), channel_id=1, source_target_pairs={{0,1},{1,2},{2,3},{3,4},{4,5},{5,6},{6,7},{7,0},{8,9},{9,10},{10,1... | collective-permute-start | bytes 1179656 | tf_op jit(solution)/shard_map/ppermute | solution.py:30
  188.9 11.6 %collective-permute-start.22 = (bf16[128,1536]{1,0:T(8,128)(2,1)}, bf16[128,1536]{1,0:T(8,128)(2,1)S(1)}, u32[]{:S(2)}, u32[]{:S(2)}) collective-permute-start(bf16[128,1536]{1,0:T(8,128)(2,1)} %get-tuple-element.150), channel_id=1, source_target_pairs={{0,7},{1,0},{2,1},{3,2},{4,3},{5,4},{6,5},{7,6},{8,15},{9,8},{10,9... | collective-permute-start | bytes 1179656 | tf_op jit(solution)/shard_map/ppermute | solution.py:35
  192.5 23.6 %collective-permute-start.15 = (bf16[192,2048]{1,0:T(8,128)(2,1)S(1)}, bf16[192,2048]{1,0:T(8,128)(2,1)}, u32[]{:S(2)}, u32[]{:S(2)}) collective-permute-start(bf16[192,2048]{1,0:T(8,128)(2,1)S(1)} %bitcast_dynamic-update-slice_fusion), channel_id=1, source_target_pairs={{0,7},{1,0},{2,1},{3,2},{4,3},{5,4},{6,5},{7,6},{8,15},{9,8},{10,9... | collective-permute-start | bytes 2359304 | tf_op jit(solution)/shard_map/ppermute | solution.py:35
  200.5 19.4 %collective-permute-start.23 = (bf16[128,1536]{1,0:T(8,128)(2,1)S(1)}, bf16[128,1536]{1,0:T(8,128)(2,1)S(1)}, u32[]{:S(2)}, u32[]{:S(2)}) collective-permute-start(bf16[128,1536]{1,0:T(8,128)(2,1)S(1)} %collective-permute-done.21), channel_id=1, source_target_pairs={{0,1},{1,2},{2,3},{3,4},{4,5},{5,6},{6,7},{7,0},{8,9},{9,10},{10,1... | collective-permute-start | bytes 1179656 | tf_op jit(solution)/shard_map/ppermute | solution.py:30
  200.5 24.0 %collective-permute-start.24 = (bf16[128,1536]{1,0:T(8,128)(2,1)S(1)}, bf16[128,1536]{1,0:T(8,128)(2,1)S(1)}, u32[]{:S(2)}, u32[]{:S(2)}) collective-permute-start(bf16[128,1536]{1,0:T(8,128)(2,1)S(1)} %collective-permute-done.22), channel_id=1, source_target_pairs={{0,7},{1,0},{2,1},{3,2},{4,3},{5,4},{6,5},{7,6},{8,15},{9,8},{10,9... | collective-permute-start | bytes 1179656 | tf_op jit(solution)/shard_map/ppermute | solution.py:35
  204.8 28.4 %collective-permute-start.16 = (bf16[192,2048]{1,0:T(8,128)(2,1)}, bf16[192,2048]{1,0:T(8,128)(2,1)S(1)}, u32[]{:S(2)}, u32[]{:S(2)}) collective-permute-start(bf16[192,2048]{1,0:T(8,128)(2,1)} %collective-permute-done.14), channel_id=1, source_target_pairs={{0,1},{1,2},{2,3},{3,4},{4,5},{5,6},{6,7},{7,0},{8,9},{9,10},{10,1... | collective-permute-start | bytes 2359304 | tf_op jit(solution)/shard_map/ppermute | solution.py:30
  216.1 34.5 %collective-permute-start.17 = (bf16[192,2048]{1,0:T(8,128)(2,1)}, bf16[192,2048]{1,0:T(8,128)(2,1)S(1)}, u32[]{:S(2)}, u32[]{:S(2)}) collective-permute-start(bf16[192,2048]{1,0:T(8,128)(2,1)} %collective-permute-done.15), channel_id=1, source_target_pairs={{0,7},{1,0},{2,1},{3,2},{4,3},{5,4},{6,5},{7,6},{8,15},{9,8},{10,9... | collective-permute-start | bytes 2359304 | tf_op jit(solution)/shard_map/ppermute | solution.py:35
  219.9 19.1 %collective-permute-start.25 = (bf16[128,1536]{1,0:T(8,128)(2,1)S(1)}, bf16[128,1536]{1,0:T(8,128)(2,1)S(1)}, u32[]{:S(2)}, u32[]{:S(2)}) collective-permute-start(bf16[128,1536]{1,0:T(8,128)(2,1)S(1)} %collective-permute-done.23), channel_id=1, source_target_pairs={{0,1},{1,2},{2,3},{3,4},{4,5},{5,6},{6,7},{7,0},{8,9},{9,10},{10,1... | collective-permute-start | bytes 1179656 | tf_op jit(solution)/shard_map/ppermute | solution.py:30
  224.5 25.3 %collective-permute-start.26 = (bf16[128,1536]{1,0:T(8,128)(2,1)S(1)}, bf16[128,1536]{1,0:T(8,128)(2,1)S(1)}, u32[]{:S(2)}, u32[]{:S(2)}) collective-permute-start(bf16[128,1536]{1,0:T(8,128)(2,1)S(1)} %collective-permute-done.24), channel_id=1, source_target_pairs={{0,7},{1,0},{2,1},{3,2},{4,3},{5,4},{6,5},{7,6},{8,15},{9,8},{10,9... | collective-permute-start | bytes 1179656 | tf_op jit(solution)/shard_map/ppermute | solution.py:35
  233.2 22.1 %collective-permute-start.18 = (bf16[192,2048]{1,0:T(8,128)(2,1)S(1)}, bf16[192,2048]{1,0:T(8,128)(2,1)S(1)}, u32[]{:S(2)}, u32[]{:S(2)}) collective-permute-start(bf16[192,2048]{1,0:T(8,128)(2,1)S(1)} %collective-permute-done.16), channel_id=1, source_target_pairs={{0,1},{1,2},{2,3},{3,4},{4,5},{5,6},{6,7},{7,0},{8,9},{9,10},{10,1... | collective-permute-start | bytes 2359304 | tf_op jit(solution)/shard_map/ppermute | solution.py:30
  239.0 21.1 %collective-permute-start.27 = (bf16[128,1536]{1,0:T(8,128)(2,1)S(1)}, bf16[128,1536]{1,0:T(8,128)(2,1)S(1)}, u32[]{:S(2)}, u32[]{:S(2)}) collective-permute-start(bf16[128,1536]{1,0:T(8,128)(2,1)S(1)} %collective-permute-done.25), channel_id=1, source_target_pairs={{0,1},{1,2},{2,3},{3,4},{4,5},{5,6},{6,7},{7,0},{8,9},{9,10},{10,1... | collective-permute-start | bytes 1179656 | tf_op jit(solution)/shard_map/ppermute | solution.py:30
  250.5 20.7 %collective-permute-start.19 = (bf16[192,2048]{1,0:T(8,128)(2,1)S(1)}, bf16[192,2048]{1,0:T(8,128)(2,1)S(1)}, u32[]{:S(2)}, u32[]{:S(2)}) collective-permute-start(bf16[192,2048]{1,0:T(8,128)(2,1)S(1)} %collective-permute-done.17), channel_id=1, source_target_pairs={{0,7},{1,0},{2,1},{3,2},{4,3},{5,4},{6,5},{7,6},{8,15},{9,8},{10,9... | collective-permute-start | bytes 2359304 | tf_op jit(solution)/shard_map/ppermute | solution.py:35
  255.3 18.7 %collective-permute-start.20 = (bf16[192,2048]{1,0:T(8,128)(2,1)S(1)}, bf16[192,2048]{1,0:T(8,128)(2,1)S(1)}, u32[]{:S(2)}, u32[]{:S(2)}) collective-permute-start(bf16[192,2048]{1,0:T(8,128)(2,1)S(1)} %collective-permute-done.18), channel_id=1, source_target_pairs={{0,1},{1,2},{2,3},{3,4},{4,5},{5,6},{6,7},{7,0},{8,9},{9,10},{10,1... | collective-permute-start | bytes 2359304 | tf_op jit(solution)/shard_map/ppermute | solution.py:30
  310.7 91.4 %all-gather.16.cloned.1.call-start = ((), (), s32[]{:S(2)}) async-start(), calls=%async_computation.16 | async-start | bytes 3932160 | tf_op jit(solution)/shard_map/all_gather | solution.py:75
  358.0 99.9 %reduce-scatter.23.cloned.1.call-start = ((), (), s32[]{:S(2)}) async-start(), calls=%async_computation.21 | async-start | bytes 3538944 | tf_op jit(solution)/shard_map/reduce_scatter | solution.py:71
  365.7 150.9 %reduce-scatter.21.cloned.1.call-start = ((), (), s32[]{:S(2)}) async-start(), calls=%async_computation.20 | async-start | bytes 7077888 | tf_op jit(solution)/shard_map/reduce_scatter | solution.py:71
  378.8 197.3 %reduce-scatter.17.cloned.1.call-start = ((), (), s32[]{:S(2)}) async-start(), calls=%async_computation.18 | async-start | bytes 5750784 | tf_op jit(solution)/shard_map/reduce_scatter | solution.py:71
  457.8 149.3 %all-gather.18.cloned.1.call-start = ((), (), s32[]{:S(2)}) async-start(), calls=%async_computation.22 | async-start | bytes 1966080 | tf_op jit(solution)/shard_map/all_gather | solution.py:292
  458.4 183.9 %reduce-scatter.19.cloned.1.call-start = ((), (), s32[]{:S(2)}) async-start(), calls=%async_computation.19 | async-start | bytes 1327104 | tf_op jit(solution)/shard_map/reduce_scatter | solution.py:71
  480.8 205.5 %all-gather.22.cloned.1.call-start = ((), (), s32[]{:S(2)}) async-start(), calls=%async_computation.24 | async-start | bytes 3932160 | tf_op jit(solution)/shard_map/all_gather | solution.py:293
  516.7 216.5 %reduce-scatter.15.cloned.1.call-start = ((), (), s32[]{:S(2)}) async-start(), calls=%async_computation.17 | async-start | bytes 3932160 | tf_op jit(solution)/shard_map/reduce_scatter | solution.py:79
  526.9 253.9 %reduce-scatter.11.cloned.1.call-start = ((), (), s32[]{:S(2)}) async-start(), calls=%async_computation.13 | async-start | bytes 3932160 | tf_op jit(solution)/shard_map/reduce_scatter | solution.py:79
  535.2 286.2 %all-gather.20.cloned.1.call-start = ((), (), s32[]{:S(2)}) async-start(), calls=%async_computation.23 | async-start | bytes 3194880 | tf_op jit(solution)/shard_map/all_gather | solution.py:297
  706.9 68.5 %copy-start.41 = (f32[256]{0:T(256)S(1)}, f32[256]{0:T(256)}, u32[]{:S(2)}) copy-start(f32[256]{0:T(256)} %copy-done.40) | copy-start | bytes 3076
  706.9 73.9 %copy-start.7 = (bf16[256,1536]{1,0:T(8,128)(2,1)S(1)}, bf16[256,1536]{1,0:T(8,128)(2,1)}, u32[]{:S(2)}) copy-start(bf16[256,1536]{1,0:T(8,128)(2,1)} %reduce-scatter.9.cloned.1.call-done) | copy-start | bytes 2359300
  706.9 73.9 %copy-start.9 = (bf16[1,256,1536]{2,1,0:T(8,128)(2,1)S(1)}, bf16[1,256,1536]{2,1,0:T(8,128)(2,1)}, u32[]{:S(2)}) copy-start(bf16[1,256,1536]{2,1,0:T(8,128)(2,1)} %param.51) | copy-start | bytes 2359300
  (59 other events, 476.8 us)
Sparse Core Ops, SparseCore 0:
  12.2 46.5 all-gather.9
  139.0 42.1 reduce-scatter.8
  183.6 43.8 all-gather.13
  229.8 43.8 all-gather.11
  310.8 42.5 reduce-scatter.12
  358.1 43.8 all-gather.15
  404.9 40.3 reduce-scatter.22
  447.6 68.9 reduce-scatter.20
  519.0 57.0 reduce-scatter.16
  577.7 29.3 all-gather.17
  609.4 32.8 reduce-scatter.18
  644.0 42.2 all-gather.21
  689.3 43.8 reduce-scatter.14
  736.0 44.6 reduce-scatter.10
  782.5 38.9 all-gather.19
